TPU v7x, 128 devices: a whole 4x4x4 slice. The times are simulated.
128 devices in a mesh: batch: 4 (over y), expert: 8 (over x, core), tensor: 4 (over z).
Axes of the slice: x: 4, y: 4, z: 4, core: 2. Of those that a mesh axis runs over, the one named last changes fastest.
Arguments:
- tokens: bfloat16 [8, 1024, 4096], P('expert', 'batch', 'tensor'), may hold values from -8 to 8
- gain: bfloat16 [4096], P('tensor'), may hold values from 0.5 to 1.5
- phi: bfloat16 [4096, 512], P('tensor'), may hold values from -1 to 1
- w_gate: bfloat16 [8, 4096, 14336], P('expert', None, ('batch', 'tensor')), may hold values from -0.125 to 0.125
- w_up: bfloat16 [8, 4096, 14336], P('expert', None, ('batch', 'tensor')), may hold values from -0.125 to 0.125
- w_down: bfloat16 [8, 14336, 4096], P('expert', ('batch', 'tensor')), may hold values from -0.09375 to 0.09375
Outputs:
- moe_out: bfloat16 [8, 1024, 4096], P('expert', 'batch', 'tensor')
All inputs are finite; a program needn't handle non-finite values.
Results may differ from a plain program's by a relative error of at most 0.025.
Values may be sent and summed in bfloat16 or wider, within the bound.
A program may use at most 128 MiB of HBM per device.

v0:
```python
import jax
import jax.numpy as jnp
from jax import lax
from jax.sharding import PartitionSpec as P

D = 4096
P_SIZE = 64


def sent_to_all(x, axis):
    size = lax.axis_size(axis)
    return lax.all_to_all(jnp.broadcast_to(x[None], (size, *x.shape)), axis, 0, 0, tiled=True)


def of_everyone(x, axis):
    return sent_to_all(x, axis).sum(axis=0)


def packed_total(arrays, axis):
    ends = [0]
    for a in arrays:
        ends.append(ends[-1] + a.size)
    running = of_everyone(jnp.concatenate([a.ravel() for a in arrays]), axis)
    return tuple((running[b:e].reshape(a.shape) for a, b, e in zip(arrays, ends, ends[1:])))


def collected_together(x, axis):
    leaves = jax.tree.leaves(x)
    order = sorted(range(len(leaves)), key=lambda k: -leaves[k].size)
    width = (1, *leaves[order[0]].shape)[-1]
    lines = [
        jnp.pad(leaves[k].reshape(-1), (0, -leaves[k].size % width)).reshape(-1, width)
        for k in order
    ]
    both, at, found = (sent_to_all(jnp.concatenate(lines), axis), 0, {})
    for k, line in zip(order, lines):
        piece = both[:, at : at + len(line)].reshape(len(both), -1)
        found[k] = piece[:, : leaves[k].size].reshape(-1, *leaves[k].shape)
        at += len(line)
    numbers = iter(range(len(leaves)))
    return jax.tree.map(lambda _: found[next(numbers)], x)


def combined_pairwise(pieces, combine):
    while len(jax.tree.leaves(pieces)[0]) > 1:
        pieces = jax.vmap(combine)(
            *(jax.tree.map(lambda part: part[side::2], pieces) for side in (0, 1))
        )
    return jax.tree.map(lambda part: part[0], pieces)


def joined_all(x, axis, combine):
    pieces = collected_together(x, axis)
    return combined_pairwise(pieces, combine)


def cut_along(x, dim, size):
    dims = x.shape
    parts = x.reshape(*dims[:dim], size, dims[dim] // size, *dims[dim + 1 :])
    return jnp.moveaxis(parts, dim, 0)


def summed_on_arrival(x, axis, dim):
    size = lax.axis_size(axis)
    parts = lax.all_to_all(cut_along(x, dim, size), axis, 0, 0, tiled=True)
    return jnp.sum(parts.astype(jnp.float32), axis=0)


def laid_out(parts, dim):
    dims = list(parts.shape[1:])
    dims[dim] *= parts.shape[0]
    return jnp.moveaxis(parts, 0, dim).reshape(dims)


def collect(x, axis, dim):
    parts = sent_to_all(x, axis)
    return laid_out(parts, dim)


def joint_totals(left_pair, right_pair):
    new_max = jnp.maximum(left_pair[0], right_pair[0])
    merged = left_pair[1] * jnp.exp(left_pair[0] - new_max) + right_pair[1] * jnp.exp(
        right_pair[0] - new_max
    )
    return (new_max, merged)


def local(tokens, gain, phi, w_gate, w_up, w_down):
    tokens_f = tokens[0].astype(jnp.float32)
    gain_f = gain.astype(jnp.float32)
    scaled = (tokens_f * gain_f[None, :]).astype(jnp.bfloat16)
    squares = jnp.sum(tokens_f * tokens_f, axis=1)
    partial_logits = jnp.dot(scaled, phi, preferred_element_type=jnp.float32)
    squares, partial_logits = packed_total((squares, partial_logits), "tensor")
    inv_rms = lax.rsqrt(squares / D + 1e-06)
    logits = partial_logits * inv_rms[:, None]
    normed = (tokens_f * gain_f[None, :] * inv_rms[:, None]).astype(jnp.bfloat16)
    combine = jax.nn.softmax(logits, axis=1).astype(jnp.bfloat16)
    local_max = jnp.max(logits, axis=0)
    local_total = jnp.sum(jnp.exp(logits - local_max[None, :]), axis=0)
    column_max, column_total = joined_all((local_max, local_total), "batch", joint_totals)
    dispatch = (jnp.exp(logits - column_max[None, :]) / column_total[None, :]).astype(jnp.bfloat16)
    slot_partial = jnp.einsum("ts,td->sd", dispatch, normed, preferred_element_type=jnp.float32)
    per_device = w_gate.shape[0]
    experts = phi.shape[1] // P_SIZE
    width_share = tokens.shape[2]
    slot_partial = slot_partial.reshape(experts, P_SIZE, width_share)
    quarter = summed_on_arrival(slot_partial.astype(jnp.bfloat16), "batch", 1).astype(jnp.bfloat16)
    exchanged = lax.all_to_all(quarter, "expert", split_axis=0, concat_axis=0, tiled=True)
    arrived = collect(exchanged, "batch", 1)
    groups = arrived.shape[0] // per_device
    arrived = arrived.reshape(groups, per_device, P_SIZE, width_share)
    hidden_share = w_gate.shape[2]
    shard_piece = lax.all_gather(arrived, "tensor", axis=3, tiled=True)
    gate_next = jnp.einsum(
        "gxpd,xdf->gxpf", shard_piece, w_gate, preferred_element_type=jnp.float32
    )
    up_next = jnp.einsum("gxpd,xdf->gxpf", shard_piece, w_up, preferred_element_type=jnp.float32)
    hidden = (jax.nn.silu(gate_next) * up_next).astype(jnp.bfloat16)
    batch_count = lax.axis_size("batch")
    tensor_count = lax.axis_size("tensor")
    hidden = hidden.reshape(groups, per_device, batch_count, P_SIZE // batch_count, hidden_share)
    down_split = w_down.reshape(per_device, hidden_share, tensor_count, D // tensor_count)
    partials = jnp.einsum(
        "gxbqf,xftd->btgxqd", hidden, down_split, preferred_element_type=jnp.float32
    )
    partials = partials.reshape(
        batch_count * tensor_count, groups, per_device, P_SIZE // batch_count, width_share
    ).astype(jnp.bfloat16)
    summed = summed_on_arrival(partials, ("batch", "tensor"), 0)
    slot_out = summed[0].astype(jnp.bfloat16)
    returned = lax.all_to_all(slot_out, "expert", split_axis=0, concat_axis=0, tiled=True)
    returned = returned.reshape(experts, P_SIZE // batch_count, width_share)
    returned = collect(returned, "batch", 1)
    moe_out = jnp.dot(
        combine, returned.reshape(experts * P_SIZE, width_share), preferred_element_type=jnp.float32
    )
    return moe_out.astype(jnp.bfloat16)[None]


def solution(mesh):
    placed = (
        P("expert", "batch", "tensor"),
        P("tensor"),
        P("tensor", None),
        P("expert", None, ("batch", "tensor")),
        P("expert", None, ("batch", "tensor")),
        P("expert", ("batch", "tensor"), None),
    )
    return jax.shard_map(
        local, mesh=mesh, in_specs=placed, out_specs=P("expert", "batch", "tensor"), check_vma=False
    )
```

profile of v0, /device:TPU:0, one launch (start us, length us, event | category | flops | bytes accessed | tf_op | source)
XLA Modules:
  0.0 282.4 jit_solution(13784396119925911884)
XLA Ops:
  6.5 0.0 copy-start
  6.5 0.0 all-gather.2.cloned.1.call-start
  6.5 1.3 fusion.22
  7.9 0.7 convert_element_type.86
  8.5 0.0 copy-done
  8.5 1.5 convolution_bitcast_fusion
  10.0 0.1 copy.46
  10.2 2.5 broadcast_in_dim.12
  12.8 31.6 %all_to_all.41 = f32[4,1,131328]{2,1,0:T(1,128)S(1)} all-to-all(f32[4,1,131328]{2,1,0:T(1,128)S(1)} %broadcast_in_dim.12), channel_id=1, replica_groups=mesh['batch'=4,'expert'=8,'tensor'=4] {'tensor'}, dimensions={0} | all-to-all | bytes 4202496 | tf_op jit(solution)/shard_map/all_to_all | solution.py:12
  44.4 0.0 copy-start.2
  44.4 10.6 %reduce_sum.61 = f32[131328]{0:T(1024)} reduce(f32[4,1,131328]{2,1,0:T(1,128)S(1)} %all_to_all.41, f32[]{:T(128)} %constant.6.clone.1), dimensions={0,1}, to_apply=%region_1.0 | reduce | flops 393984 | bytes 2626564 | tf_op jit(solution)/shard_map/reduce_sum | solution.py:16
  55.0 0.7 fusion.35
  55.7 1.1 slice.52
  56.7 0.1 reshape.121
  56.8 0.2 multiply_reduce_fusion
  57.0 0.3 exponential_reduce_fusion
  57.4 9.6 %all_to_all.42 = f32[4,2,512]{2,1,0:T(2,128)S(1)} all-to-all(f32[4,2,512]{2,1,0:T(2,128)S(1)} %broadcast_in_dim.13), channel_id=1, replica_groups=mesh['batch'=4,'expert'=8,'tensor'=4] {'batch'}, dimensions={0} | all-to-all | bytes 32768 | tf_op jit(solution)/shard_map/all_to_all | solution.py:12
  67.2 0.2 fusion.32
  67.4 0.1 copy.31
  67.5 0.0 copy-done.2
  67.5 0.5 convolution_convert_fusion
  68.0 0.1 copy.57
  68.1 15.2 %all_to_all.43 = bf16[4,8,16,1024]{3,2,1,0:T(8,128)(2,1)S(1)} all-to-all(bf16[4,8,16,1024]{3,2,1,0:T(8,128)(2,1)S(1)} %bitcast.118), channel_id=1, replica_groups=mesh['batch'=4,'expert'=8,'tensor'=4] {'batch'}, dimensions={0} | all-to-all | bytes 2097152 | tf_op jit(solution)/shard_map/all_to_all | solution.py:65
  83.3 0.2 reduce_sum.64
  83.5 11.6 %all_to_all.44 = bf16[8,16,1024]{2,1,0:T(8,128)(2,1)S(1)} all-to-all(bf16[8,16,1024]{2,1,0:T(8,128)(2,1)S(1)} %reduce_sum.64), channel_id=1, replica_groups=mesh['batch'=4,'expert'=8,'tensor'=4] {'expert'}, dimensions={0} | all-to-all | bytes 524288 | tf_op jit(solution)/shard_map/all_to_all | solution.py:109
  95.1 0.1 broadcast_in_dim.14
  95.2 17.4 %all_to_all.45 = bf16[4,8,16,1024]{3,2,1,0:T(8,128)(2,1)S(1)} all-to-all(bf16[4,8,16,1024]{3,2,1,0:T(8,128)(2,1)S(1)} %broadcast_in_dim.14), channel_id=1, replica_groups=mesh['batch'=4,'expert'=8,'tensor'=4] {'batch'}, dimensions={0} | all-to-all | bytes 2097152 | tf_op jit(solution)/shard_map/all_to_all | solution.py:12
  112.6 1.0 copy.33
  113.7 0.0 all-gather.2.cloned.1.call-update
  113.7 13.1 %reshape.131 = bf16[896,4,1024]{2,1,0:T(4,128)(2,1)} reshape(bf16[1,896,4096]{2,1,0:T(8,128)(2,1)} %param.11) | data formatting | bytes 14680064 | tf_op jit(solution)/shard_map/reshape.6
  126.8 31.1 %all-gather.2.cloned.1.call-done = bf16[8,1,64,4096]{3,2,0,1:T(8,128)(2,1)} async-done(((bf16[8,1,64,1024]{3,2,0,1:T(8,128)(2,1)}), bf16[8,1,64,4096]{3,2,0,1:T(8,128)(2,1)}) %all-gather.2.cloned.1.call-update) | async-done | bytes 4194320 | tf_op jit(solution)/shard_map/all_gather | solution.py:114
  157.9 0.0 copy-start.4
  157.9 0.0 slice-start
  157.9 10.5 %fusion.4 = f32[8,64,896]{2,1,0:T(8,128)S(1)} fusion(bf16[1,4096,896]{2,1,0:T(8,128)(2,1)} %param.9, bf16[8,1,64,4096]{3,2,0,1:T(8,128)(2,1)} %all-gather.2.cloned.1.call-done), kind=kOutput, calls=%fused_computation.4 | convolution fusion | flops 3758096384 | bytes 13369344 | tf_op jit(solution)/shard_map/gxpd,xdf->gxpf/dot_general | solution.py:115
  168.5 0.0 copy-done.4
  168.5 0.0 slice-start.1
  168.5 7.8 %fusion.11 = bf16[8,1,64,896]{3,2,0,1:T(8,128)(2,1)S(1)} fusion(f32[8,64,896]{2,1,0:T(8,128)S(1)} %fusion.4, bf16[1,4096,896]{2,1,0:T(8,128)(2,1)} %param.10, bf16[8,1,64,4096]{3,2,0,1:T(8,128)(2,1)S(1)} %copy-done.4), kind=kOutput, calls=%fused_computation.10 | convolution fusion | flops 3760848896 | bytes 14286848 | tf_op jit(solution)/shard_map/gxpd,xdf->gxpf/dot_general | solution.py:118
  176.2 0.0 slice-done
  176.2 0.0 slice-done.1
  176.3 5.6 %fusion.8 = bf16[8,4,16,4,1024]{4,2,3,1,0:T(8,128)(2,1)S(1)} fusion(bf16[8,4,16,896,1]{3,2,4,1,0:T(8,128)(2,1)S(1)} %bitcast.130, bf16[896,4,1024,1,1]{2,1,0,4,3:T(4,128)(2,1)S(1)} %bitcast.113), kind=kOutput, calls=%fused_computation.8 | convolution fusion | flops 3760193536 | bytes 12451840 | tf_op jit(solution)/shard_map/gxbqf,xftd->btgxqd/dot_general | solution.py:124
  181.9 0.4 copy.35
  182.4 56.5 %all_to_all.46 = bf16[16,1,8,1,16,1024]{5,4,2,3,1,0:T(8,128)(2,1)} all-to-all(bf16[16,1,8,1,16,1024]{5,4,2,3,1,0:T(8,128)(2,1)S(1)} %copy.35), channel_id=1, replica_groups=mesh['batch'=4,'expert'=8,'tensor'=4] {'batch','tensor'}, dimensions={0} | all-to-all | bytes 8388608 | tf_op jit(solution)/shard_map/all_to_all | solution.py:65
  238.8 3.9 %reduce_sum.65 = bf16[8,16,1024]{2,1,0:T(8,128)(2,1)} reduce(bf16[16,1,8,1,16,1024]{5,4,2,3,1,0:T(8,128)(2,1)} %all_to_all.46, bf16[]{:T(256)} %constant.15.clone.1), dimensions={0,1,3}, to_apply=%region_7.8 | reduce | flops 1966080 | bytes 4456450 | tf_op jit(solution)/shard_map/reduce_sum | solution.py:66
  242.7 0.0 copy-start.3
  242.7 4.4 %all-to-all-start.6 = ((bf16[8,1,16,1024]{3,2,1,0:T(8,128)(2,1)}), bf16[8,1,16,1024]{3,2,1,0:T(8,128)(2,1)S(1)}, u32[]{:S(2)}, u32[]{:S(2)}) async-start(bf16[8,1,16,1024]{3,2,1,0:T(8,128)(2,1)} %bitcast.35), calls=%async_computation.6 | async-start | bytes 524288 | tf_op jit(solution)/shard_map/all_to_all | solution.py:132
  247.1 0.1 broadcast_bitcast_fusion
  247.2 0.9 copy.49
  248.1 1.0 copy.48
  249.1 0.9 copy.47
  250.0 4.6 %all-to-all-done.6 = bf16[8,1,16,1024]{3,2,1,0:T(8,128)(2,1)S(1)} async-done(((bf16[8,1,16,1024]{3,2,1,0:T(8,128)(2,1)}), bf16[8,1,16,1024]{3,2,1,0:T(8,128)(2,1)S(1)}, u32[]{:S(2)}, u32[]{:S(2)}) %all-to-all-start.6) | async-done | bytes 262176 | tf_op jit(solution)/shard_map/all_to_all | solution.py:132
  254.6 0.0 copy-start.1
  254.6 1.1 broadcast_in_dim.16
  255.7 3.5 %all-to-all-start.7 = ((bf16[4,8,16,1024]{3,2,1,0:T(8,128)(2,1)}), bf16[4,8,16,1024]{3,2,1,0:T(8,128)(2,1)S(1)}, u32[]{:S(2)}, u32[]{:S(2)}) async-start(bf16[4,8,16,1024]{3,2,1,0:T(8,128)(2,1)} %broadcast_in_dim.16), calls=%async_computation.7 | async-start | bytes 2097152 | tf_op jit(solution)/shard_map/all_to_all | solution.py:12
  259.2 0.0 copy-done.3
  259.3 1.5 divide_convert_fusion.1
  260.8 0.2 convert_element_type.89
  260.9 13.3 %all-to-all-done.7 = bf16[4,8,16,1024]{3,2,1,0:T(8,128)(2,1)S(1)} async-done(((bf16[4,8,16,1024]{3,2,1,0:T(8,128)(2,1)}), bf16[4,8,16,1024]{3,2,1,0:T(8,128)(2,1)S(1)}, u32[]{:S(2)}, u32[]{:S(2)}) %all-to-all-start.7) | async-done | bytes 1048608 | tf_op jit(solution)/shard_map/all_to_all | solution.py:12
  274.2 0.1 copy.36
  274.3 1.2 fusion.21
  275.6 0.0 copy-done.1
  (12 shorter events, 0.2 us)
Async XLA Ops:
  6.5 2.0 copy-start
  6.5 151.4 %all-gather.2.cloned.1.call-start = ((), (), s32[]{:S(2)}) async-start(), calls=%async_computation.8 | async-start | bytes 5242880 | tf_op jit(solution)/shard_map/all_gather | solution.py:114
  44.4 23.1 %copy-start.2 = (bf16[1,256,1024]{2,1,0:T(8,128)(2,1)S(1)}, bf16[1,256,1024]{2,1,0:T(8,128)(2,1)}, u32[]{:S(2)}) copy-start(bf16[1,256,1024]{2,1,0:T(8,128)(2,1)} %param.6) | copy-start | bytes 1572868
  157.9 10.5 %copy-start.4 = (bf16[8,1,64,4096]{3,2,0,1:T(8,128)(2,1)S(1)}, bf16[8,1,64,4096]{3,2,0,1:T(8,128)(2,1)}, u32[]{:S(2)}) copy-start(bf16[8,1,64,4096]{3,2,0,1:T(8,128)(2,1)} %all-gather.2.cloned.1.call-done) | copy-start | bytes 12582916
  157.9 18.3 %slice-start = ((s8[7340032]{0:T(1024)(128)(4,1)}), s8[4194304]{0:T(1024)(128)(4,1)S(1)}, s32[]{:S(2)}) async-start(s8[7340032]{0:T(1024)(128)(4,1)} %bitcast.111), calls=%async_computation.9 | async-start | bytes 8388608
  168.5 7.8 %slice-start.1 = ((s8[7340032]{0:T(1024)(128)(4,1)}), s8[3145728]{0:T(1024)(128)(4,1)S(1)}, s32[]{:S(2)}) async-start(s8[7340032]{0:T(1024)(128)(4,1)} %bitcast.111), calls=%async_computation.10 | async-start | bytes 6291456
  242.7 16.5 %copy-start.3 = (f32[131328]{0:T(1024)S(1)}, f32[131328]{0:T(1024)}, u32[]{:S(2)}) copy-start(f32[131328]{0:T(1024)} %reduce_sum.61) | copy-start | bytes 1575940
  242.7 11.9 %all-to-all-start.6 = ((bf16[8,1,16,1024]{3,2,1,0:T(8,128)(2,1)}), bf16[8,1,16,1024]{3,2,1,0:T(8,128)(2,1)S(1)}, u32[]{:S(2)}, u32[]{:S(2)}) async-start(bf16[8,1,16,1024]{3,2,1,0:T(8,128)(2,1)} %bitcast.35), calls=%async_computation.6 | async-start | bytes 524288 | tf_op jit(solution)/shard_map/all_to_all | solution.py:132
  254.6 21.0 %copy-start.1 = (bf16[1024,512]{1,0:T(8,128)(2,1)S(1)}, bf16[1024,512]{1,0:T(8,128)(2,1)}, u32[]{:S(2)}) copy-start(bf16[1024,512]{1,0:T(8,128)(2,1)} %param.8) | copy-start | bytes 3145732
  255.7 18.5 %all-to-all-start.7 = ((bf16[4,8,16,1024]{3,2,1,0:T(8,128)(2,1)}), bf16[4,8,16,1024]{3,2,1,0:T(8,128)(2,1)S(1)}, u32[]{:S(2)}, u32[]{:S(2)}) async-start(bf16[4,8,16,1024]{3,2,1,0:T(8,128)(2,1)} %broadcast_in_dim.16), calls=%async_computation.7 | async-start | bytes 2097152 | tf_op jit(solution)/shard_map/all_to_all | solution.py:12
Sparse Core Ops, SparseCore 0:
  113.8 44.0 all-gather.1
where the time goes:
time: 283 us; the launch traced here: 282 us
  blocking collectives  142 us (50%)
  waiting for transfers between devices  49 us (17%)
  matrix products  27.2 us (10%)
  local copies, waits for them, and re-layouts  23.2 us (8%)
  other arithmetic  19.6 us (7%)
  between operations  13.7 us (5%)
  starting transfers between devices  7.9 us (3%)
    all_to_all x2, blocking collectives, summed_on_arrival(): parts = lax.all_to_all(cut_along(x, dim, size), axis, 0, 0, tiled=True)  71.6 us
    all_to_all x3, blocking collectives, sent_to_all(): lax.all_to_all(jnp.broadcast_to(x[None], (size, *x.shape)), axis, 0, 0, t...  58.7 us
    all_gather x1, waiting for transfers between devices, local(): shard_piece = lax.all_gather(arrived, 'tensor', axis=3, tiled=True)  31.1 us
    all_to_all x1, waiting for transfers between devices, sent_to_all(): lax.all_to_all(jnp.broadcast_to(x[None], (size, *x.shape)), axis, 0, 0, t...  13.3 us
    another operation x1, local copies, waits for them, and re-layouts  13.1 us
    all_to_all x1, blocking collectives, local(): lax.all_to_all(quarter, 'expert', split_axis=0, concat_axis=0, tiled=True)  11.6 us
    reduce_sum x1, other arithmetic, of_everyone(): return sent_to_all(x, axis).sum(axis=0)  10.6 us
    dot_general x1, matrix products, local(): jnp.einsum('gxpd,xdf->gxpf', shard_piece, w_gate, preferred_element_type=...  10.5 us
  transfers between devices with their start and end apart: 3, of which 3 were waited for; matrix products, arithmetic and copies ran while one was open for 6% of the time, Pallas kernels for 0%

commit v1 on v0

--- a/solution.py
+++ b/solution.py
@@ -5,6 +5,25 @@
 
 D = 4096
 P_SIZE = 64
+
+
+def gather_around(shard, axis, dim):
+    size, place, span = (lax.axis_size(axis), lax.axis_index(axis), shard.shape[dim])
+    ahead = [(i, (i + 1) % size) for i in range(size)]
+    backward = [(i, (i - 1) % size) for i in range(size)]
+    out = jnp.zeros((*shard.shape[:dim], size * span, *shard.shape[dim + 1 :]), shard.dtype)
+    out = lax.dynamic_update_slice_in_dim(out, shard, place * span, axis=dim)
+    from_left = from_right = shard
+    halfway = size // 2
+    for lap in range(1, halfway + 1):
+        from_left = lax.ppermute(from_left, axis, ahead)
+        out = lax.dynamic_update_slice_in_dim(out, from_left, (place - lap) % size * span, axis=dim)
+        if lap < size - halfway:
+            from_right = lax.ppermute(from_right, axis, backward)
+            out = lax.dynamic_update_slice_in_dim(
+                out, from_right, (place + lap) % size * span, axis=dim
+            )
+    return out
 
 
 def sent_to_all(x, axis):
@@ -111,7 +130,7 @@
     groups = arrived.shape[0] // per_device
     arrived = arrived.reshape(groups, per_device, P_SIZE, width_share)
     hidden_share = w_gate.shape[2]
-    shard_piece = lax.all_gather(arrived, "tensor", axis=3, tiled=True)
+    shard_piece = gather_around(arrived, "tensor", 3)
     gate_next = jnp.einsum(
         "gxpd,xdf->gxpf", shard_piece, w_gate, preferred_element_type=jnp.float32
     )

time: 283 us -> 265 us (0.936)
  between operations: 13.7 us -> 0.35 us
  matrix products: 27.2 us -> 22.1 us
  blocking collectives: 142 us -> 137 us
    all_gather x1 -> x0, waiting for transfers between devices: 31.1 us -> none  [local(): shard_piece = lax.all_gather(arrived, 'tensor', axis=3, tiled=True)]
    ppermute x0 -> x3, waiting for transfers between devices: none -> 30.9 us  [the longest x2 30.9 us: gather_around(): from_left = lax.ppermute(from_left, axis, ahead)]
    all_to_all x2, blocking collectives: 71.6 us -> 66.5 us  [summed_on_arrival(): parts = lax.all_to_all(cut_along(x, dim, size), axis, 0, 0, tiled=True)]
    ppermute x0 -> x3, starting transfers between devices: none -> 3.31 us  [the longest x1 2.67 us: gather_around(): from_right = lax.ppermute(from_right, axis, backward)]
    dot_general x1, matrix products: 7.75 us -> 4.59 us  [local(): jnp.einsum('gxpd,xdf->gxpf', shard_piece, w_up, preferred_element_type=jn...]
    dynamic_update_slice x0 -> x4, local copies, waits for them, and re-layouts: none -> 3.04 us  [the longest x2 1.59 us: gather_around(): lax.dynamic_update_slice_in_dim(out, from_left, (place - lap) % size * sp...]
    another operation x1 -> x2, local copies, waits for them, and re-layouts: 13.1 us -> 13.3 us
  transfers between devices with their start and end apart: 3 -> 5, of which waited for: 3 -> 4; matrix products, arithmetic and copies ran while one was open for 6% -> 7% of each run, Pallas kernels for 0% -> 0%
where the time goes in v1:
time: 265 us; the launch traced here: 264 us
  blocking collectives  137 us (52%)
  waiting for transfers between devices  48.7 us (18%)
  local copies, waits for them, and re-layouts  25.5 us (10%)
  matrix products  22.1 us (8%)
  other arithmetic  19.6 us (7%)
  starting transfers between devices  10.6 us (4%)
    all_to_all x2, blocking collectives, summed_on_arrival(): parts = lax.all_to_all(cut_along(x, dim, size), axis, 0, 0, tiled=True)  66.5 us
    all_to_all x3, blocking collectives, sent_to_all(): lax.all_to_all(jnp.broadcast_to(x[None], (size, *x.shape)), axis, 0, 0, t...  58.7 us
    ppermute x2, waiting for transfers between devices, gather_around(): from_left = lax.ppermute(from_left, axis, ahead)  30.9 us
    another operation x2, local copies, waits for them, and re-layouts  13.3 us
    all_to_all x1, waiting for transfers between devices, sent_to_all(): lax.all_to_all(jnp.broadcast_to(x[None], (size, *x.shape)), axis, 0, 0, t...  13.3 us
    all_to_all x1, blocking collectives, local(): lax.all_to_all(quarter, 'expert', split_axis=0, concat_axis=0, tiled=True)  11.6 us
    reduce_sum x1, other arithmetic, of_everyone(): return sent_to_all(x, axis).sum(axis=0)  10.5 us
    dot_general x1, matrix products, local(): jnp.einsum('gxpd,xdf->gxpf', shard_piece, w_gate, preferred_element_type=...  8.68 us
  transfers between devices with their start and end apart: 5, of which 4 were waited for; matrix products, arithmetic and copies ran while one was open for 7% of the time, Pallas kernels for 0%

profile of v1, /device:TPU:0, one launch (start us, length us, event | category | flops | bytes accessed | tf_op | source)
XLA Modules:
  0.0 263.7 jit_solution(7778050350489611703)
XLA Ops:
  0.0 0.8 convert_element_type.86
  0.8 1.2 fusion.18
  2.0 1.5 convolution_bitcast_fusion
  3.5 0.1 copy.52
  3.7 2.5 broadcast_in_dim.12
  6.2 31.6 %all_to_all.41 = f32[4,1,131328]{2,1,0:T(1,128)S(1)} all-to-all(f32[4,1,131328]{2,1,0:T(1,128)S(1)} %broadcast_in_dim.12), channel_id=1, replica_groups=mesh['batch'=4,'expert'=8,'tensor'=4] {'tensor'}, dimensions={0} | all-to-all | bytes 4202496 | tf_op jit(solution)/shard_map/all_to_all | solution.py:31
  37.9 10.5 %reduce_sum.61 = f32[131328]{0:T(1024)} reduce(f32[4,1,131328]{2,1,0:T(1,128)S(1)} %all_to_all.41, f32[]{:T(128)} %constant.43.clone.1), dimensions={0,1}, to_apply=%region_1.0 | reduce | flops 393984 | bytes 2626564 | tf_op jit(solution)/shard_map/reduce_sum | solution.py:35
  48.4 1.1 slice.52
  49.5 0.7 fusion.31
  50.2 0.1 reshape.136
  50.2 0.2 multiply_reduce_fusion
  50.4 0.3 exponential_reduce_fusion
  50.8 9.6 %all_to_all.42 = f32[4,2,512]{2,1,0:T(2,128)S(1)} all-to-all(f32[4,2,512]{2,1,0:T(2,128)S(1)} %broadcast_in_dim.13), channel_id=1, replica_groups=mesh['batch'=4,'expert'=8,'tensor'=4] {'batch'}, dimensions={0} | all-to-all | bytes 32768 | tf_op jit(solution)/shard_map/all_to_all | solution.py:31
  60.6 0.2 fusion.28
  60.8 0.1 copy.37
  60.9 0.0 copy-done.2
  60.9 0.5 convolution_convert_fusion
  61.4 0.1 copy.63
  61.5 15.2 %all_to_all.43 = bf16[4,8,16,1024]{3,2,1,0:T(8,128)(2,1)S(1)} all-to-all(bf16[4,8,16,1024]{3,2,1,0:T(8,128)(2,1)S(1)} %bitcast.124), channel_id=1, replica_groups=mesh['batch'=4,'expert'=8,'tensor'=4] {'batch'}, dimensions={0} | all-to-all | bytes 2097152 | tf_op jit(solution)/shard_map/all_to_all | solution.py:84
  76.7 0.2 reduce_sum.64
  76.9 11.6 %all_to_all.44 = bf16[8,16,1024]{2,1,0:T(8,128)(2,1)S(1)} all-to-all(bf16[8,16,1024]{2,1,0:T(8,128)(2,1)S(1)} %reduce_sum.64), channel_id=1, replica_groups=mesh['batch'=4,'expert'=8,'tensor'=4] {'expert'}, dimensions={0} | all-to-all | bytes 524288 | tf_op jit(solution)/shard_map/all_to_all | solution.py:128
  88.5 0.1 broadcast_in_dim.14
  88.6 17.4 %all_to_all.45 = bf16[4,8,16,1024]{3,2,1,0:T(8,128)(2,1)S(1)} all-to-all(bf16[4,8,16,1024]{3,2,1,0:T(8,128)(2,1)S(1)} %broadcast_in_dim.14), channel_id=1, replica_groups=mesh['batch'=4,'expert'=8,'tensor'=4] {'batch'}, dimensions={0} | all-to-all | bytes 2097152 | tf_op jit(solution)/shard_map/all_to_all | solution.py:31
  106.1 0.1 copy.39
  106.1 0.6 collective-permute-start
  106.8 2.7 %collective-permute-start.1 = (bf16[8,1,64,1024]{3,2,0,1:T(8,128)(2,1)S(1)}, bf16[8,1,64,1024]{3,2,0,1:T(8,128)(2,1)}, u32[]{:S(2)}, u32[]{:S(2)}) collective-permute-start(bf16[8,1,64,1024]{3,2,0,1:T(8,128)(2,1)S(1)} %bitcast.119), channel_id=1, source_target_pairs={{0,3},{1,0},{2,1},{3,2},{4,7},{5,4},{6,5},{7,6},{8,11},{9,8},{10,9... | collective-permute-start | bytes 3145736 | tf_op jit(solution)/shard_map/ppermute | solution.py:22
  109.4 21.6 %collective-permute-done = bf16[8,1,64,1024]{3,2,0,1:T(8,128)(2,1)S(1)} collective-permute-done((bf16[8,1,64,1024]{3,2,0,1:T(8,128)(2,1)S(1)}, bf16[8,1,64,1024]{3,2,0,1:T(8,128)(2,1)S(1)}, u32[]{:S(2)}, u32[]{:S(2)}) %collective-permute-start) | collective-permute-done | bytes 1048608 | tf_op jit(solution)/shard_map/ppermute | solution.py:19
  131.1 0.0 collective-permute-start.2
  131.1 12.8 %reshape.149 = bf16[896,4,1024]{2,1,0:T(4,128)(2,1)} reshape(bf16[1,896,4096]{2,1,0:T(8,128)(2,1)} %param.11) | data formatting | bytes 14680064 | tf_op jit(solution)/shard_map/reshape.6
  143.9 0.5 broadcast.40
  144.4 0.1 constant_dynamic-update-slice_fusion
  144.6 0.1 bitcast_dynamic-update-slice_fusion.2
  144.7 0.0 collective-permute-done.1
  144.7 1.3 bitcast_dynamic-update-slice_fusion.1
  146.0 9.2 %collective-permute-done.2 = bf16[8,1,64,1024]{3,2,0,1:T(8,128)(2,1)} collective-permute-done((bf16[8,1,64,1024]{3,2,0,1:T(8,128)(2,1)S(1)}, bf16[8,1,64,1024]{3,2,0,1:T(8,128)(2,1)}, u32[]{:S(2)}, u32[]{:S(2)}) %collective-permute-start.2) | collective-permute-done | bytes 1048608 | tf_op jit(solution)/shard_map/ppermute | solution.py:19
  155.2 1.5 bitcast_dynamic-update-slice_fusion
  156.7 0.0 slice-start.3
  156.7 0.0 slice-start
  156.7 8.7 %fusion.4 = f32[8,64,896]{2,1,0:T(8,128)S(1)} fusion(bf16[8,64,4096]{2,1,0:T(8,128)(2,1)S(1)} %bitcast_dynamic-update-slice_fusion, bf16[1,4096,896]{2,1,0:T(8,128)(2,1)} %param.9), kind=kOutput, calls=%fused_computation.4 | convolution fusion | flops 3758096384 | bytes 13369344 | tf_op jit(solution)/shard_map/gxpd,xdf->gxpf/dot_general | solution.py:134
  165.4 0.0 slice-done.2
  165.4 0.0 slice-done.3
  165.5 0.0 slice-start.1
  165.5 4.6 %fusion.9 = bf16[8,1,64,896]{3,2,0,1:T(8,128)(2,1)S(1)} fusion(f32[8,64,896]{2,1,0:T(8,128)S(1)} %fusion.4, bf16[8,64,4096]{2,1,0:T(8,128)(2,1)S(1)} %bitcast_dynamic-update-slice_fusion, bf16[1,4096,896]{2,1,0:T(8,128)(2,1)S(1)} %bitcast.136), kind=kOutput, calls=%fused_computation.8 | convolution fusion | flops 3760848896 | bytes 14286848 | tf_op jit(solution)/shard_map/gxpd,xdf->gxpf/dot_general | solution.py:137
  170.1 0.0 slice-done
  170.1 0.0 slice-done.1
  170.1 5.6 %fusion.6 = bf16[8,4,16,4,1024]{4,2,3,1,0:T(8,128)(2,1)S(1)} fusion(bf16[8,4,16,896,1]{3,2,4,1,0:T(8,128)(2,1)S(1)} %bitcast.137, bf16[896,4,1024,1,1]{2,1,0,4,3:T(4,128)(2,1)S(1)} %bitcast.117), kind=kOutput, calls=%fused_computation.6 | convolution fusion | flops 3760193536 | bytes 12451840 | tf_op jit(solution)/shard_map/gxbqf,xftd->btgxqd/dot_general | solution.py:143
  175.7 0.4 copy.41
  176.2 51.4 %all_to_all.46 = bf16[16,1,8,1,16,1024]{5,4,2,3,1,0:T(8,128)(2,1)} all-to-all(bf16[16,1,8,1,16,1024]{5,4,2,3,1,0:T(8,128)(2,1)S(1)} %copy.41), channel_id=1, replica_groups=mesh['batch'=4,'expert'=8,'tensor'=4] {'batch','tensor'}, dimensions={0} | all-to-all | bytes 8388608 | tf_op jit(solution)/shard_map/all_to_all | solution.py:84
  227.6 3.9 %reduce_sum.65 = bf16[8,16,1024]{2,1,0:T(8,128)(2,1)} reduce(bf16[16,1,8,1,16,1024]{5,4,2,3,1,0:T(8,128)(2,1)} %all_to_all.46, bf16[]{:T(256)} %constant.47.clone.1), dimensions={0,1,3}, to_apply=%region_7.8 | reduce | flops 1966080 | bytes 4456450 | tf_op jit(solution)/shard_map/reduce_sum | solution.py:85
  231.4 3.8 %all-to-all-start.6 = ((bf16[8,1,16,1024]{3,2,1,0:T(8,128)(2,1)}), bf16[8,1,16,1024]{3,2,1,0:T(8,128)(2,1)S(1)}, u32[]{:S(2)}, u32[]{:S(2)}) async-start(bf16[8,1,16,1024]{3,2,1,0:T(8,128)(2,1)} %bitcast.39), calls=%async_computation.6 | async-start | bytes 524288 | tf_op jit(solution)/shard_map/all_to_all | solution.py:151
  235.2 0.1 broadcast_bitcast_fusion
  235.4 0.9 copy.55
  236.3 0.9 copy.54
  237.2 0.9 copy.53
  238.1 4.6 %all-to-all-done.6 = bf16[8,1,16,1024]{3,2,1,0:T(8,128)(2,1)S(1)} async-done(((bf16[8,1,16,1024]{3,2,1,0:T(8,128)(2,1)}), bf16[8,1,16,1024]{3,2,1,0:T(8,128)(2,1)S(1)}, u32[]{:S(2)}, u32[]{:S(2)}) %all-to-all-start.6) | async-done | bytes 262176 | tf_op jit(solution)/shard_map/all_to_all | solution.py:151
  242.8 1.1 broadcast_in_dim.16
  243.9 3.5 %all-to-all-start.7 = ((bf16[4,8,16,1024]{3,2,1,0:T(8,128)(2,1)}), bf16[4,8,16,1024]{3,2,1,0:T(8,128)(2,1)S(1)}, u32[]{:S(2)}, u32[]{:S(2)}) async-start(bf16[4,8,16,1024]{3,2,1,0:T(8,128)(2,1)} %broadcast_in_dim.16), calls=%async_computation.7 | async-start | bytes 2097152 | tf_op jit(solution)/shard_map/all_to_all | solution.py:31
  247.4 0.0 copy-done.3
  247.4 1.5 divide_convert_fusion.1
  248.9 0.2 convert_element_type.89
  249.1 13.3 %all-to-all-done.7 = bf16[4,8,16,1024]{3,2,1,0:T(8,128)(2,1)S(1)} async-done(((bf16[4,8,16,1024]{3,2,1,0:T(8,128)(2,1)}), bf16[4,8,16,1024]{3,2,1,0:T(8,128)(2,1)S(1)}, u32[]{:S(2)}, u32[]{:S(2)}) %all-to-all-start.7) | async-done | bytes 1048608 | tf_op jit(solution)/shard_map/all_to_all | solution.py:31
  262.4 0.1 copy.42
  262.5 1.2 fusion.17
  263.7 0.0 copy-done.1
  (19 shorter events, 0.2 us)
Async XLA Ops:
  0.0 2.0 copy-start
  37.8 23.1 %copy-start.2 = (bf16[1,256,1024]{2,1,0:T(8,128)(2,1)S(1)}, bf16[1,256,1024]{2,1,0:T(8,128)(2,1)}, u32[]{:S(2)}) copy-start(bf16[1,256,1024]{2,1,0:T(8,128)(2,1)} %param.6) | copy-start | bytes 1572868
  106.1 25.0 %collective-permute-start = (bf16[8,1,64,1024]{3,2,0,1:T(8,128)(2,1)S(1)}, bf16[8,1,64,1024]{3,2,0,1:T(8,128)(2,1)S(1)}, u32[]{:S(2)}, u32[]{:S(2)}) collective-permute-start(bf16[8,1,64,1024]{3,2,0,1:T(8,128)(2,1)S(1)} %bitcast.118), channel_id=1, source_target_pairs={{0,1},{1,2},{2,3},{3,0},{4,5},{5,6},{6,7},{7,4},{8,9},{9,10},{10,1... | collective-permute-start | bytes 3145736 | tf_op jit(solution)/shard_map/ppermute | solution.py:19
  106.8 37.9 %collective-permute-start.1 = (bf16[8,1,64,1024]{3,2,0,1:T(8,128)(2,1)S(1)}, bf16[8,1,64,1024]{3,2,0,1:T(8,128)(2,1)}, u32[]{:S(2)}, u32[]{:S(2)}) collective-permute-start(bf16[8,1,64,1024]{3,2,0,1:T(8,128)(2,1)S(1)} %bitcast.119), channel_id=1, source_target_pairs={{0,3},{1,0},{2,1},{3,2},{4,7},{5,4},{6,5},{7,6},{8,11},{9,8},{10,9... | collective-permute-start | bytes 3145736 | tf_op jit(solution)/shard_map/ppermute | solution.py:22
  131.1 24.1 %collective-permute-start.2 = (bf16[8,1,64,1024]{3,2,0,1:T(8,128)(2,1)S(1)}, bf16[8,1,64,1024]{3,2,0,1:T(8,128)(2,1)}, u32[]{:S(2)}, u32[]{:S(2)}) collective-permute-start(bf16[8,1,64,1024]{3,2,0,1:T(8,128)(2,1)S(1)} %collective-permute-done), channel_id=1, source_target_pairs={{0,1},{1,2},{2,3},{3,0},{4,5},{5,6},{6,7},{7,4},{8,9},{9,10},{10,1... | collective-permute-start | bytes 3145736 | tf_op jit(solution)/shard_map/ppermute | solution.py:19
  155.2 10.2 %slice-start.2 = ((s8[7340032]{0:T(1024)(128)(4,1)}), s8[4194304]{0:T(1024)(128)(4,1)S(1)}, s32[]{:S(2)}) async-start(s8[7340032]{0:T(1024)(128)(4,1)} %bitcast.135), calls=%async_computation.10 | async-start | bytes 8388608
  156.7 8.7 %slice-start.3 = ((s8[7340032]{0:T(1024)(128)(4,1)}), s8[3145728]{0:T(1024)(128)(4,1)S(1)}, s32[]{:S(2)}) async-start(s8[7340032]{0:T(1024)(128)(4,1)} %bitcast.135), calls=%async_computation.11 | async-start | bytes 6291456
  156.7 13.3 %slice-start = ((s8[7340032]{0:T(1024)(128)(4,1)}), s8[4194304]{0:T(1024)(128)(4,1)S(1)}, s32[]{:S(2)}) async-start(s8[7340032]{0:T(1024)(128)(4,1)} %bitcast.115), calls=%async_computation.8 | async-start | bytes 8388608
  165.5 4.6 %slice-start.1 = ((s8[7340032]{0:T(1024)(128)(4,1)}), s8[3145728]{0:T(1024)(128)(4,1)S(1)}, s32[]{:S(2)}) async-start(s8[7340032]{0:T(1024)(128)(4,1)} %bitcast.115), calls=%async_computation.9 | async-start | bytes 6291456
  231.4 15.9 %copy-start.3 = (f32[131328]{0:T(1024)S(1)}, f32[131328]{0:T(1024)}, u32[]{:S(2)}) copy-start(f32[131328]{0:T(1024)} %reduce_sum.61) | copy-start | bytes 1575940
  231.4 11.3 %all-to-all-start.6 = ((bf16[8,1,16,1024]{3,2,1,0:T(8,128)(2,1)}), bf16[8,1,16,1024]{3,2,1,0:T(8,128)(2,1)S(1)}, u32[]{:S(2)}, u32[]{:S(2)}) async-start(bf16[8,1,16,1024]{3,2,1,0:T(8,128)(2,1)} %bitcast.39), calls=%async_computation.6 | async-start | bytes 524288 | tf_op jit(solution)/shard_map/all_to_all | solution.py:151
  242.8 21.0 %copy-start.1 = (bf16[1024,512]{1,0:T(8,128)(2,1)S(1)}, bf16[1024,512]{1,0:T(8,128)(2,1)}, u32[]{:S(2)}) copy-start(bf16[1024,512]{1,0:T(8,128)(2,1)} %param.8) | copy-start | bytes 3145732
  243.9 18.5 %all-to-all-start.7 = ((bf16[4,8,16,1024]{3,2,1,0:T(8,128)(2,1)}), bf16[4,8,16,1024]{3,2,1,0:T(8,128)(2,1)S(1)}, u32[]{:S(2)}, u32[]{:S(2)}) async-start(bf16[4,8,16,1024]{3,2,1,0:T(8,128)(2,1)} %broadcast_in_dim.16), calls=%async_computation.7 | async-start | bytes 2097152 | tf_op jit(solution)/shard_map/all_to_all | solution.py:31
